TPU v7x, 128 devices: a whole 4x4x4 slice. The times are simulated.
128 devices in a mesh: batch: 1, col: 16 (over z, y), row: 8 (over x, core).
Axes of the slice: x: 4, y: 4, z: 4, core: 2. Of those that a mesh axis runs over, the one named last changes fastest.
Arguments:
- lower_tri: float32 [6144, 6144], P(('batch', 'row'), 'col')
Outputs:
- output: float32 [6144, 6144], P(('batch', 'row'), 'col')
All inputs are finite; a program needn't handle non-finite values.
Results may differ from a plain program's by a relative error of at most 0.001.
Values sent between devices are 32-bit elements.
A program may use at most 1 GiB of HBM per device.

v0:
```python
import jax
import jax.numpy as jnp
from jax import lax
from jax.sharding import PartitionSpec as P

LEAF_MAX = 512
HIGHEST = lax.Precision.HIGHEST


def leaf_plan(order_n):
    depth_n = 0
    leaf_n = order_n
    while leaf_n > LEAF_MAX:
        leaf_n = leaf_n // 2
        depth_n = depth_n + 1
    return depth_n, leaf_n


def tile_size(order_n, leaf_n, count_n):
    return min(leaf_n // count_n, order_n // (count_n * count_n))


def rows_to_cyclic(local_blk, count_n, tile_n):
    rows_n, cols_n = local_blk.shape
    shaped = local_blk.reshape(rows_n // (count_n * tile_n), count_n, tile_n, cols_n)
    swapped = lax.all_to_all(shaped, "row", 1, 0)
    return swapped.reshape(rows_n, cols_n)


def cols_to_cyclic(local_blk, count_n, tile_n):
    rows_n, cols_n = local_blk.shape
    shaped = local_blk.reshape(rows_n, cols_n // (count_n * tile_n), count_n, tile_n)
    swapped = lax.all_to_all(shaped, "col", 2, 1)
    return swapped.reshape(rows_n, cols_n)


def rows_to_block(local_blk, count_n, tile_n):
    rows_n, cols_n = local_blk.shape
    shaped = local_blk.reshape(count_n, rows_n // (count_n * tile_n), tile_n, cols_n)
    swapped = lax.all_to_all(shaped, "row", 0, 1)
    return swapped.reshape(rows_n, cols_n)


def cols_to_block(local_blk, count_n, tile_n):
    rows_n, cols_n = local_blk.shape
    shaped = local_blk.reshape(rows_n, count_n, cols_n // (count_n * tile_n), tile_n)
    swapped = lax.all_to_all(shaped, "col", 1, 2)
    return swapped.reshape(rows_n, cols_n)


def gather_cols(pieces, count_n, tile_n):
    blocks_n, rows_n, cols_n = pieces.shape
    shaped = pieces.reshape(blocks_n, rows_n, cols_n // tile_n, tile_n)
    full_pan = lax.all_gather(shaped, "col", axis=3)
    return full_pan.reshape(blocks_n, rows_n, cols_n * count_n)


def gather_rows(pieces, count_n, tile_n):
    blocks_n, rows_n, cols_n = pieces.shape
    shaped = pieces.reshape(blocks_n, rows_n // tile_n, tile_n, cols_n)
    full_pan = lax.all_gather(shaped, "row", axis=2)
    return full_pan.reshape(blocks_n, rows_n * count_n, cols_n)


def diag_blocks(local_blk, count_n):
    rows_n, cols_n = local_blk.shape
    block_grid = local_blk.reshape(count_n, rows_n // count_n, count_n, cols_n // count_n)
    picked = jnp.diagonal(block_grid, axis1=0, axis2=2)
    return jnp.moveaxis(picked, 2, 0)


def leaf_inverses(leaf_pieces, count_r, count_c, tile_r, tile_c):
    leaves_n, piece_r, piece_c = leaf_pieces.shape
    leaf_n = piece_r * count_r
    whole_leaf = gather_rows(gather_cols(leaf_pieces, count_c, tile_c), count_r, tile_r)
    col_pos = lax.axis_index("col")
    row_pos = lax.axis_index("row")
    local_cols = jnp.arange(piece_c)
    global_cols = (local_cols // tile_c) * (count_c * tile_c) + col_pos * tile_c + local_cols % tile_c
    unit_cols = (jnp.arange(leaf_n)[:, None] == global_cols[None, :]).astype(jnp.float32)
    rhs_cols = jnp.broadcast_to(unit_cols, (leaves_n, leaf_n, piece_c))
    solved = lax.linalg.triangular_solve(whole_leaf, rhs_cols, left_side=True, lower=True)
    shaped = solved.reshape(leaves_n, piece_r // tile_r, count_r, tile_r, piece_c)
    own_rows = lax.dynamic_index_in_dim(shaped, row_pos, axis=2, keepdims=False)
    return own_rows.reshape(leaves_n, piece_r, piece_c)


def assemble(inv_a, inv_b, low_x):
    top_half = jnp.concatenate([inv_a, jnp.zeros_like(inv_a)], axis=2)
    bottom = jnp.concatenate([low_x, inv_b], axis=2)
    return jnp.concatenate([top_half, bottom], axis=1)


def solution(mesh):
    count_r = mesh.shape["row"]
    count_c = mesh.shape["col"]

    def local_fn(tri_block):
        rows_loc, cols_loc = tri_block.shape
        order_n = cols_loc * count_c
        depth_n, leaf_n = leaf_plan(order_n)
        tile_r = tile_size(order_n, leaf_n, count_r)
        tile_c = tile_size(order_n, leaf_n, count_c)
        tri_cyc = cols_to_cyclic(rows_to_cyclic(tri_block, count_r, tile_r), count_c, tile_c)
        leaf_pieces = diag_blocks(tri_cyc, 2 ** depth_n)
        inv_diag = leaf_inverses(leaf_pieces, count_r, count_c, tile_r, tile_c)
        for level_k in range(depth_n - 1, -1, -1):
            blocks_n = 2 ** level_k
            half_r = rows_loc // (2 * blocks_n)
            half_c = cols_loc // (2 * blocks_n)
            low_c = diag_blocks(tri_cyc, blocks_n)[:, half_r:, :half_c]
            inv_pairs = inv_diag.reshape(blocks_n, 2, half_r, half_c)
            c_rows = gather_cols(low_c, count_c, tile_c)
            a_cols = gather_rows(inv_pairs[:, 0], count_r, tile_r)
            prod_t = jnp.einsum("jab,jbc->jac", c_rows, a_cols, precision=HIGHEST, preferred_element_type=jnp.float32)
            b_rows = gather_cols(inv_pairs[:, 1], count_c, tile_c)
            t_cols = gather_rows(prod_t, count_r, tile_r)
            low_x = -jnp.einsum("jab,jbc->jac", b_rows, t_cols, precision=HIGHEST, preferred_element_type=jnp.float32)
            inv_diag = assemble(inv_pairs[:, 0], inv_pairs[:, 1], low_x)
        inv_cyc = inv_diag[0]
        x_rows = gather_cols(inv_diag, count_c, tile_c)[0]
        split_a = x_rows.reshape(rows_loc, order_n // (count_r * tile_r), count_r, tile_r)
        part_sum = jnp.einsum("tkrb,tc->krbc", split_a, inv_cyc, precision=HIGHEST, preferred_element_type=jnp.float32)
        summed = lax.psum_scatter(part_sum, "row", scatter_dimension=1, tiled=False)
        out_cyc = summed.reshape(rows_loc, cols_loc)
        return cols_to_block(rows_to_block(out_cyc, count_r, tile_r), count_c, tile_c)

    block_spec = P(("batch", "row"), "col")
    return jax.shard_map(local_fn, mesh=mesh, in_specs=(block_spec,), out_specs=block_spec, check_vma=False)
```

profile of v0, /device:TPU:1, one launch (start us, length us, event | category | flops | bytes accessed | tf_op | source)
XLA Modules:
  0.0 1491.8 jit_solution(10435503670909603828)
XLA Ops:
  7.9 22.1 %all_to_all.48 = f32[1,2,8,48,384]{4,3,1,0,2:T(8,128)S(1)} all-to-all(f32[1,2,8,48,384]{4,3,1,0,2:T(8,128)S(1)} %copy.159), channel_id=1, replica_groups=mesh['batch'=1,'col'=16,'row'=8] {'row'}, dimensions={2} | all-to-all | bytes 2359296 | tf_op jit(solution)/shard_map/all_to_all | solution.py:26
  48.2 17.0 %all-to-all-done.1 = f32[768,1,1,16,24]{0,4,2,1,3:T(8,128)S(1)} async-done(((f32[768,1,1,16,24]{0,4,2,1,3:T(8,128)}), f32[768,1,1,16,24]{0,4,2,1,3:T(8,128)S(1)}, u32[]{:S(2)}, u32[]{:S(2)}) %all-to-all-start.1) | async-done | bytes 1179680 | tf_op jit(solution)/shard_map/all_to_all | solution.py:33
  75.7 44.9 %all-gather.41.cloned.1.call-done = f32[16,48,384]{1,0,2:T(8,128)} async-done(((f32[16,48,24]{1,0,2:T(8,128)}), f32[16,48,384]{1,0,2:T(8,128)}) %all-gather.41.cloned.1.call-update) | async-done | bytes 1179664 | tf_op jit(solution)/shard_map/all_gather | solution.py:54
  133.7 23.6 %all-gather.2 = f32[8,48,384]{1,2,0:T(8,128)S(1)} all-gather(f32[8,48,24]{1,2,0:T(8,128)S(1)} %slice.98), channel_id=4, replica_groups=mesh['batch'=1,'col'=16,'row'=8] {'col'}, dimensions={2}, use_global_device_ids=true | all-gather | bytes 626688 | tf_op jit(solution)/shard_map/all_gather | solution.py:54
  157.6 20.8 %all-gather.45.cloned.1.call-done = f32[16,384,384]{2,1,0:T(8,128)} async-done(((f32[16,48,384]{2,1,0:T(8,128)}), f32[16,384,384]{2,1,0:T(8,128)}) %all-gather.45.cloned.1.call-update) | async-done | bytes 9437200 | tf_op jit(solution)/shard_map/all_gather | solution.py:61
  201.0 473.0 %custom-call.3 = f32[16,3,128,128]{2,3,1,0:T(8,128)} custom-call(f32[16,3,128,128]{3,2,1,0:T(8,128)} %bitcast.239), custom_call_target="InvertDiagBlocksLowerTriangular" | custom-call | tf_op jit(solution)/shard_map/triangular_solve | solution.py:82
  709.0 21.3 %all-gather.1 = f32[8,1,48,384]{2,0,1,3:T(8,128)S(1)} all-gather(f32[8,1,48,24]{2,0,1,3:T(8,128)S(1)} %copy.172), channel_id=3, replica_groups=mesh['batch'=1,'col'=16,'row'=8] {'col'}, dimensions={3}, use_global_device_ids=true | all-gather | bytes 626688 | tf_op jit(solution)/shard_map/all_gather | solution.py:54
  730.8 20.2 %all-gather.4 = f32[8,384,24]{2,0,1:T(8,128)S(1)} all-gather(f32[8,48,24]{2,0,1:T(8,128)S(1)} %copy.176), channel_id=6, replica_groups=mesh['batch'=1,'col'=16,'row'=8] {'row'}, dimensions={1}, use_global_device_ids=true | all-gather | bytes 331776 | tf_op jit(solution)/shard_map/all_gather | solution.py:61
  757.0 15.3 %all_gather.65 = f32[4,2,8,48,48]{4,3,1,0,2:T(8,128)S(1)} all-gather(f32[4,2,1,48,48]{4,3,1,0,2:T(8,128)S(1)} %bitcast.232), channel_id=1, replica_groups=mesh['batch'=1,'col'=16,'row'=8] {'row'}, dimensions={2}, use_global_device_ids=true | all-gather | bytes 663552 | tf_op jit(solution)/shard_map/all_gather | solution.py:61
  780.2 15.7 %all_gather.66 = f32[4,2,8,48,48]{4,3,1,0,2:T(8,128)S(1)} all-gather(f32[4,2,1,48,48]{4,3,1,0,2:T(8,128)S(1)} %bitcast.230), channel_id=1, replica_groups=mesh['batch'=1,'col'=16,'row'=8] {'row'}, dimensions={2}, use_global_device_ids=true | all-gather | bytes 663552 | tf_op jit(solution)/shard_map/all_gather | solution.py:61
  804.1 38.8 %all-gather.27.cloned.1.call-done = f32[2,192,4,16,24]{1,4,2,0,3:T(8,128)} async-done(((f32[2,192,4,1,24]{1,4,2,0,3:T(8,128)}), f32[2,192,4,16,24]{1,4,2,0,3:T(8,128)}) %all-gather.27.cloned.1.call-update) | async-done | bytes 2359312 | tf_op jit(solution)/shard_map/all_gather | solution.py:54
  846.8 22.5 %all-gather.29.cloned.1.call-done = f32[2,4,8,48,96]{4,3,1,0,2:T(8,128)} async-done(((f32[2,4,1,48,96]{4,3,1,0,2:T(8,128)}), f32[2,4,8,48,96]{4,3,1,0,2:T(8,128)}) %all-gather.29.cloned.1.call-update) | async-done | bytes 1179664 | tf_op jit(solution)/shard_map/all_gather | solution.py:61
  879.2 23.0 %all-gather.31.cloned.1.call-done = f32[2,4,8,48,96]{4,3,2,1,0:T(8,128)} async-done(((f32[2,4,1,48,96]{4,3,2,1,0:T(8,128)}), f32[2,4,8,48,96]{4,3,2,1,0:T(8,128)}) %all-gather.31.cloned.1.call-update) | async-done | bytes 1179664 | tf_op jit(solution)/shard_map/all_gather | solution.py:61
  902.2 48.3 %all-gather.25.cloned.1.call-done = f32[2,192,4,16,24]{1,4,3,2,0:T(8,128)} async-done(((f32[2,192,4,1,24]{1,4,3,2,0:T(8,128)}), f32[2,192,4,16,24]{1,4,3,2,0:T(8,128)}) %all-gather.25.cloned.1.call-update) | async-done | bytes 2359312 | tf_op jit(solution)/shard_map/all_gather | solution.py:54
  958.1 48.3 %all-gather.35.cloned.1.call-done = f32[1,384,8,16,24]{1,4,3,2,0:T(8,128)} async-done(((f32[1,384,8,1,24]{1,4,3,2,0:T(8,128)}), f32[1,384,8,16,24]{1,4,3,2,0:T(8,128)}) %all-gather.35.cloned.1.call-update) | async-done | bytes 4718608 | tf_op jit(solution)/shard_map/all_gather | solution.py:54
  1016.8 18.8 %all-gather.37.cloned.1.call-done = f32[1,8,8,48,192]{4,3,1,0,2:T(8,128)} async-done(((f32[1,8,1,48,192]{4,3,1,0,2:T(8,128)}), f32[1,8,8,48,192]{4,3,1,0,2:T(8,128)}) %all-gather.37.cloned.1.call-update) | async-done | bytes 2359312 | tf_op jit(solution)/shard_map/all_gather | solution.py:61
  1037.7 25.2 %fusion.6 = f32[8,48,192]{2,1,0:T(8,128)} fusion(f32[3072,192,1]{1,0,2:T(8,128)S(1)} %bitcast.207, f32[8,48,3072]{1,0,2:T(8,128)} %reshape.137), kind=kOutput, calls=%fused_computation.15 | convolution fusion | flops 2717908992 | bytes 7372800 | tf_op jit(solution)/shard_map/jab,jbc->jac/dot_general | solution.py:115
  1063.5 27.1 %all-gather.43.cloned.1.call-done = f32[8,384,192]{2,1,0:T(8,128)} async-done(((f32[8,48,192]{2,1,0:T(8,128)}), f32[8,384,192]{2,1,0:T(8,128)}) %all-gather.43.cloned.1.call-update) | async-done | bytes 2359312 | tf_op jit(solution)/shard_map/all_gather | solution.py:61
  1090.6 55.2 %all-gather.33.cloned.1.call-done = f32[1,384,8,16,24]{1,4,3,2,0:T(8,128)} async-done(((f32[1,384,8,1,24]{1,4,3,2,0:T(8,128)}), f32[1,384,8,16,24]{1,4,3,2,0:T(8,128)}) %all-gather.33.cloned.1.call-update) | async-done | bytes 4718608 | tf_op jit(solution)/shard_map/all_gather | solution.py:54
  1156.5 121.5 %all-gather.39.cloned.1.call-done = f32[1,768,16,16,24]{1,4,2,0,3:T(8,128)} async-done(((f32[1,768,16,1,24]{1,4,2,0,3:T(8,128)}), f32[1,768,16,16,24]{1,4,2,0,3:T(8,128)}) %all-gather.39.cloned.1.call-update) | async-done | bytes 18874384 | tf_op jit(solution)/shard_map/all_gather | solution.py:54
  1285.2 32.1 %fusion.9 = f32[16,8,48,384]{3,2,1,0:T(8,128)} fusion(f32[768,16,8,48]{0,3,2,1:T(8,128)S(1)} %bitcast.204, f32[1,384,192]{1,2,0:T(8,128)S(1)} %get-tuple-element.28, f32[1,384,192]{1,2,0:T(8,128)S(1)} %get-tuple-element.29, f32[1,384,192]{1,2,0:T(8,128)S(1)} %fusion.11), kind=kOutput, calls=%fused_computation.18 | convolution fusion | flops 21744451584 | bytes 29196288 | tf_op jit(solution)/shard_map/tkrb,tc->krbc/dot_general | solution.py:123
  1318.5 112.3 %all-reduce.7.cloned.1.call-done = f32[16,8,48,384]{3,2,1,0:T(8,128)} async-done(((f32[16,8,48,384]{3,2,1,0:T(8,128)}), f32[16,8,48,384]{3,2,1,0:T(8,128)}) %all-reduce.7.cloned.1.call-update) | async-done | bytes 9437200
  1432.8 20.1 %all_to_all.49 = f32[8,2,1,48,384]{4,3,2,1,0:T(8,128)S(1)} all-to-all(f32[8,2,1,48,384]{4,3,2,1,0:T(8,128)S(1)} %bitcast.211), channel_id=1, replica_groups=mesh['batch'=1,'col'=16,'row'=8] {'row'}, dimensions={0} | all-to-all | bytes 2359296 | tf_op jit(solution)/shard_map/all_to_all | solution.py:40
  1457.9 25.8 %all_to_all.50 = f32[768,16,1,1,24]{0,4,3,2,1:T(8,128)S(1)} all-to-all(f32[768,16,1,1,24]{0,4,3,2,1:T(8,128)S(1)} %bitcast.217), channel_id=1, replica_groups=mesh['batch'=1,'col'=16,'row'=8] {'col'}, dimensions={1} | all-to-all | bytes 2359296 | tf_op jit(solution)/shard_map/all_to_all | solution.py:47
  (137 shorter events, 199.3 us)
Async XLA Ops:
  40.3 24.8 %all-to-all-start.1 = ((f32[768,1,1,16,24]{0,4,2,1,3:T(8,128)}), f32[768,1,1,16,24]{0,4,2,1,3:T(8,128)S(1)}, u32[]{:S(2)}, u32[]{:S(2)}) async-start(f32[768,1,1,16,24]{0,4,2,1,3:T(8,128)} %bitcast.3), calls=%async_computation.1 | async-start | bytes 2359296 | tf_op jit(solution)/shard_map/all_to_all | solution.py:33
  48.1 72.5 %all-gather.41.cloned.1.call-start = ((), (), s32[]{:S(2)}) async-start(), calls=%async_computation.14 | async-start | bytes 3342336 | tf_op jit(solution)/shard_map/all_gather | solution.py:54
  75.6 102.8 %all-gather.45.cloned.1.call-start = ((), (), s32[]{:S(2)}) async-start(), calls=%async_computation.16 | async-start | bytes 10616832 | tf_op jit(solution)/shard_map/all_gather | solution.py:61
  123.7 652.4 %all-gather.23.cloned.1.call-start = ((), (), s32[]{:S(2)}) async-start(), calls=%async_computation.5 | async-start | bytes 1671168 | tf_op jit(solution)/shard_map/all_gather | solution.py:54
  157.4 642.3 %all-gather.21.cloned.1.call-start = ((), (), s32[]{:S(2)}) async-start(), calls=%async_computation.4 | async-start | bytes 1671168 | tf_op jit(solution)/shard_map/all_gather | solution.py:54
  706.7 2.3 copy-start.2
  751.0 2.6 copy-start.5
  751.0 2.6 copy-start.6
  754.5 88.4 %all-gather.27.cloned.1.call-start = ((), (), s32[]{:S(2)}) async-start(), calls=%async_computation.7 | async-start | bytes 3342336 | tf_op jit(solution)/shard_map/all_gather | solution.py:54
  755.3 1.5 copy-start.1
  756.8 112.5 %all-gather.29.cloned.1.call-start = ((), (), s32[]{:S(2)}) async-start(), calls=%async_computation.8 | async-start | bytes 1769472 | tf_op jit(solution)/shard_map/all_gather | solution.py:61
  799.7 2.6 copy-start.3
  799.7 2.6 copy-start.4
  804.0 98.2 %all-gather.31.cloned.1.call-start = ((), (), s32[]{:S(2)}) async-start(), calls=%async_computation.9 | async-start | bytes 1769472 | tf_op jit(solution)/shard_map/all_gather | solution.py:61
  869.3 2.4 copy-start
  877.6 73.0 %all-gather.25.cloned.1.call-start = ((), (), s32[]{:S(2)}) async-start(), calls=%async_computation.6 | async-start | bytes 3342336 | tf_op jit(solution)/shard_map/all_gather | solution.py:54
  878.3 128.0 %all-gather.35.cloned.1.call-start = ((), (), s32[]{:S(2)}) async-start(), calls=%async_computation.11 | async-start | bytes 5013504 | tf_op jit(solution)/shard_map/all_gather | solution.py:54
  879.2 156.4 %all-gather.37.cloned.1.call-start = ((), (), s32[]{:S(2)}) async-start(), calls=%async_computation.12 | async-start | bytes 3538944 | tf_op jit(solution)/shard_map/all_gather | solution.py:61
  957.6 133.0 %all-gather.43.cloned.1.call-start = ((), (), s32[]{:S(2)}) async-start(), calls=%async_computation.15 | async-start | bytes 3538944 | tf_op jit(solution)/shard_map/all_gather | solution.py:61
  1062.8 82.9 %all-gather.33.cloned.1.call-start = ((), (), s32[]{:S(2)}) async-start(), calls=%async_computation.10 | async-start | bytes 5013504 | tf_op jit(solution)/shard_map/all_gather | solution.py:54
  1063.4 214.6 %all-gather.39.cloned.1.call-start = ((), (), s32[]{:S(2)}) async-start(), calls=%async_computation.13 | async-start | bytes 20054016 | tf_op jit(solution)/shard_map/all_gather | solution.py:54
  1156.3 274.5 %all-reduce.7.cloned.1.call-start = ((), (), s32[]{:S(2)}) async-start(), calls=%async_computation.17 | async-start | bytes 18874368
  1317.2 0.7 copy-start.7
Sparse Core Ops, SparseCore 0:
  75.7 44.7 all-gather.40
  123.9 54.4 all-gather.44
  180.6 41.7 all-gather.22
  754.7 38.4 all-gather.20
  795.1 47.7 all-gather.26
  844.4 24.8 all-gather.28
  877.7 24.4 all-gather.30
  904.4 46.1 all-gather.24
  952.8 53.5 all-gather.34
  1007.9 27.6 all-gather.36
  1063.0 27.5 all-gather.42
  1092.6 53.0 all-gather.32
  1156.4 121.5 all-gather.38
  1317.4 113.3 all-reduce.6
where the time goes:
time: 1500 us; the launch traced here: 1490 us
  waiting for transfers between devices  600 us (40%)
  other arithmetic  483 us (32%)
  blocking collectives  178 us (12%)
  local copies, waits for them, and re-layouts  106 us (7%)
  matrix products  102 us (7%)
    another operation x5, other arithmetic, leaf_inverses(): lax.linalg.triangular_solve(whole_leaf, rhs_cols, left_side=True, lower=T...  482 us
    all_gather x8, waiting for transfers between devices, gather_cols(): full_pan = lax.all_gather(shaped, 'col', axis=3)  357 us
    unnamed x15, waiting for transfers between devices  114 us
    all_gather x5, waiting for transfers between devices, gather_rows(): full_pan = lax.all_gather(shaped, 'row', axis=2)  112 us
    all_gather x4, blocking collectives, gather_rows(): full_pan = lax.all_gather(shaped, 'row', axis=2)  65.1 us
    all_gather x2, blocking collectives, gather_cols(): full_pan = lax.all_gather(shaped, 'col', axis=3)  44.9 us
    dot_general x3, matrix products, local_fn(): jnp.einsum('jab,jbc->jac', c_rows, a_cols, precision=HIGHEST, preferred_e...  33.2 us
    dot_general x1, matrix products, local_fn(): jnp.einsum('tkrb,tc->krbc', split_a, inv_cyc, precision=HIGHEST, preferre...  32.1 us
  transfers between devices with their start and end apart: 15, of which 13 were waited for; matrix products, arithmetic and copies ran while one was open for 38% of the time, Pallas kernels for 0%

commit v1 on v0

v1 whole, which is shorter than its diff:
```python
import functools

import jax
import jax.numpy as jnp
from jax import lax
from jax.experimental import pallas as pl
from jax.experimental.pallas import tpu as pltpu
from jax.sharding import PartitionSpec as P

MESH = pl.DeviceIdType.MESH
HIGHEST = lax.Precision.HIGHEST
F32 = jnp.float32
VMEM_LIMIT = 60 * 1024 * 1024
BASE = 128


def coords():
    col = lax.axis_index("col")
    row = lax.axis_index("row")
    return {"x": row // 2, "y": col % 4, "z": col // 4, "e": row % 2}


def device(at):
    return (0, 4 * at["z"] + at["y"], 2 * at["x"] + at["e"])


def same(p, q):
    return (p["x"] == q["x"]) & (p["y"] == q["y"]) & (p["z"] == q["z"]) & (p["e"] == q["e"])


def mm(a, b, dims=((1,), (0,))):
    return lax.dot_general(a, b, (dims, ((), ())), precision=HIGHEST, preferred_element_type=F32)


def push(src, dst, send_sem, recv_sem, to, me):
    here = same(to, me)

    @pl.when(here)
    def _():
        dst[...] = src[...]

    @pl.when(jnp.logical_not(here))
    def _():
        pltpu.make_async_remote_copy(
            src_ref=src, dst_ref=dst, send_sem=send_sem, recv_sem=recv_sem, device_id=device(to), device_id_type=MESH
        ).start()


def sent(src, dst, send_sem, recv_sem, to, me):
    @pl.when(jnp.logical_not(same(to, me)))
    def _():
        pltpu.make_async_remote_copy(
            src_ref=src, dst_ref=dst, send_sem=send_sem, recv_sem=recv_sem, device_id=device(to), device_id_type=MESH
        ).wait_send()


def arrived(dst, send_sem, recv_sem, source, me):
    @pl.when(jnp.logical_not(same(source, me)))
    def _():
        pltpu.make_async_remote_copy(
            src_ref=dst, dst_ref=dst, send_sem=send_sem, recv_sem=recv_sem, device_id=device(source), device_id_type=MESH
        ).wait_recv()


def meet(sources, dests, me):
    barrier = pltpu.get_barrier_semaphore()

    def other(cond, at):
        apart = jnp.logical_not(same(at, me))
        return apart if cond is None else apart & cond

    for cond, at in sources:
        @pl.when(other(cond, at))
        def _(at=at):
            pl.semaphore_signal(barrier, inc=1, device_id=device(at), device_id_type=MESH)

    total = sum(other(cond, at).astype(jnp.int32) for cond, at in dests)

    @pl.when(total > 0)
    def _():
        pl.semaphore_wait(barrier, total)


def invert_block(left, corner, inv, base):
    half = 3 * base
    rows = lax.broadcasted_iota(jnp.int32, (base, base), 0)
    cols = lax.broadcasted_iota(jnp.int32, (base, base), 1)
    eye = rows == cols

    def block(i, j):
        if j < 3:
            return left[i * base:(i + 1) * base, j * base:(j + 1) * base]
        return corner[(i - 3) * base:(i - 2) * base, (j - 3) * base:(j - 2) * base]

    tri = [block(i, i) for i in range(6)]
    found = []
    for i in range(6):
        diag = jnp.sum(jnp.where(eye, tri[i], 0.0), axis=1, keepdims=True)
        found.append(jnp.where(eye, 1.0 / diag, 0.0))
    size = 1
    while size < base:
        below = ((rows // size) % 2 == 1) & (cols // size == rows // size - 1)
        half_way = [mm(jnp.where(below, tri[i], 0.0), found[i]) for i in range(6)]
        found = [found[i] - mm(found[i], half_way[i]) for i in range(6)]
        size = size * 2
    inv[...] = jnp.zeros(inv.shape, F32)
    for k in (0, 3):
        x0, x1, x2 = found[k:k + 3]
        x10 = -mm(x1, mm(block(k + 1, k), x0))
        x21 = -mm(x2, mm(block(k + 2, k + 1), x1))
        x20 = -mm(x2, mm(block(k + 2, k), x0) + mm(block(k + 2, k + 1), x10))
        for i, j, val in ((0, 0, x0), (1, 1, x1), (2, 2, x2), (1, 0, x10), (2, 1, x21), (2, 0, x20)):
            inv[(k + i) * base:(k + i + 1) * base, (k + j) * base:(k + j + 1) * base] = val
    low = mm(left[half:, :], inv[:half, :half])
    inv[half:, :half] = -mm(inv[half:, half:], low)


def stage0_kernel(n, l_ref, lt_ref, ct_out, d_out, g_out, dt_out,
                  left, corner, cmat, inv_a, inv_b, inv_t, slab_d, slab_t, slab_g,
                  ct_send, ct_recv, ab_send, ab_recv, c_send, c_recv, x_send, x_recv, t_send, t_recv):
    me = coords()
    x, y, z, e = me["x"], me["y"], me["z"], me["e"]
    big = n // 8
    half = n // 16
    quarter = n // 32
    tile = n // 128
    sib = dict(me, e=1 - e)
    diag = x == z

    slot = (x * (x - 1)) // 2 + z
    hops = [(ee, g, h) for g in range(4) for ee in range(2) for h in range(2)]

    def ct_args(ee, g, h):
        src = lt_ref.at[pl.ds(quarter * ee + tile * g, tile), pl.ds(half * h, half)]
        to = {"x": jnp.int32(g), "y": y, "z": 2 * e + h, "e": jnp.int32(ee)}
        return src, ct_out.at[slot], ct_send.at[ee * 8 + g * 2 + h], ct_recv.at[slot], to, me

    source = diag & (y // 2 == e)
    c_source = diag & (e == 1) & (y < 2)

    def at(b, along_y):
        return {"x": jnp.int32(b), "y": along_y, "z": jnp.int32(b), "e": e}

    odd = x % 2

    def dest(kind, g, j):
        if kind == 0:
            return {"x": jnp.int32(j), "y": y, "z": jnp.int32(g), "e": e}
        if kind == 1:
            return {"x": odd * g + (1 - odd) * j, "y": odd * j + (1 - odd) * g, "z": y, "e": e}
        return {"x": jnp.int32(g), "y": jnp.int32(j), "z": y, "e": e}

    every = [(kind, g, j) for kind in range(3) for g in range(4) for j in range(4)]
    pairs = [(b_row, b_col) for b_row in range(4) for b_col in range(b_row)]

    def ct_source(b_row, b_col):
        return {"x": jnp.int32(b_row), "y": y, "z": jnp.int32(b_col), "e": z // 2}

    sources = [(None, ct_source(*pair)) for pair in pairs] + [(diag, sib)]
    sources += [(diag, dict(me, y=2 * e + part)) for part in range(2)]
    sources += [(diag & (e == 1), dict(me, y=jnp.int32(part))) for part in range(2)]
    sources += [(None, at(b, v)) for b in range(4) for v in (y, z)] + [(None, at(1, z))]
    dests = [(x > z, ct_args(*hop)[4]) for hop in hops] + [(diag, sib)]
    dests += [(cond, dict(me, y=(y + k) % 4)) for cond in (source, c_source) for k in range(1, 4)]
    dests += [(diag if kind < 2 else diag & (x == 1), dest(kind, g, j)) for kind, g, j in every]
    meet(sources, dests, me)

    def ab_args(k, part):
        to = dict(me, y=(y + k) % 4)
        if part == 0:
            return l_ref, left, ab_send.at[k - 1], ab_recv.at[0], to, me
        return l_ref.at[pl.ds(half, half), :], corner, ab_send.at[k - 1], ab_recv.at[1], to, me

    for part in range(2):
        @pl.when(source & (y % 2 == part))
        def _(part=part):
            for k in (1, 3, 2):
                push(*ab_args(k, part))

    def c_args(k):
        to = dict(me, y=(y + k) % 4)
        return l_ref, cmat.at[y % 2], c_send.at[k - 1], c_recv.at[y % 2], to, me

    @pl.when(c_source)
    def _():
        for k in (1, 3, 2):
            push(*c_args(k))

    @pl.when(x > z)
    def _():
        for hop in hops:
            push(*ct_args(*hop))

    def swap_args(k):
        mine = [inv_a, inv_b, cmat.at[0], cmat.at[1]][k]
        return mine, mine, x_send.at[k], x_recv.at[k], sib, me

    @pl.when(diag)
    def _():
        for part, (dst, src_rows) in enumerate(((left, 0), (corner, half))):
            @pl.when(source & (y % 2 == part))
            def _(dst=dst, src_rows=src_rows):
                dst[...] = l_ref[src_rows:, :]

            arrived(dst, ab_send.at[0], ab_recv.at[part], dict(me, y=2 * e + part), me)

        invert_block(left, corner, inv_t, n // 48)
        for core, inv in ((0, inv_a), (1, inv_b)):
            @pl.when(e == core)
            def _(inv=inv):
                inv[...] = inv_t[...]

        @pl.when(e == 0)
        def _():
            push(*swap_args(0))
            for k in (1, 2, 3):
                arrived(swap_args(k)[1], x_send.at[k], x_recv.at[k], sib, me)
            sent(*swap_args(0))

        @pl.when(e == 1)
        def _():
            push(*swap_args(1))
            for part in range(2):
                @pl.when(y == part)
                def _(part=part):
                    cmat[part] = l_ref[...]

                arrived(cmat.at[part], c_send.at[0], c_recv.at[part], dict(me, y=jnp.int32(part)), me)
                push(*swap_args(2 + part))
            arrived(inv_a, x_send.at[0], x_recv.at[0], sib, me)
            for k in (1, 2, 3):
                sent(*swap_args(k))

        first = pl.multiple_of((y % 2) * half + e * quarter, 8)
        mine = pl.ds(first, quarter)

        def times_c(v):
            return jnp.concatenate([mm(v, cmat[0]), mm(v, cmat[1])], axis=1)

        @pl.when(y < 2)
        def _():
            slab_d[:, :big] = inv_a[mine, :]
            slab_d[:, big:] = jnp.zeros((quarter, big), F32)
            inv_t[...] = inv_a[...].T
            u_a = inv_t[mine, :]
            slab_t[:, :big] = u_a
            w = mm(u_a[:, :half], cmat[0], ((1,), (1,))) + mm(u_a[:, half:], cmat[1], ((1,), (1,)))
            slab_t[:, big:] = -mm(w, inv_b[...], ((1,), (1,)))
            q = mm(slab_t[:, big:], inv_b[...])
            slab_g[:, big:] = q
            slab_g[:, :big] = mm(slab_t[:, :big] - times_c(q), inv_a[...])

        @pl.when(y >= 2)
        def _():
            v_b = inv_b[mine, :]
            slab_d[:, big:] = v_b
            slab_d[:, :big] = -mm(times_c(v_b), inv_a[...])
            inv_t[...] = inv_b[...].T
            u_b = inv_t[mine, :]
            slab_t[:, :big] = jnp.zeros((quarter, big), F32)
            slab_t[:, big:] = u_b
            q = mm(u_b, inv_b[...])
            slab_g[:, big:] = q
            slab_g[:, :big] = -mm(times_c(q), inv_a[...])

        def spread(kind, g, j):
            rows, cols = pl.ds(tile * g, tile), pl.ds(half * j, half)
            src = (slab_d, slab_g, slab_t)[kind].at[rows, cols]
            dst = (d_out, g_out)[kind].at[x] if kind < 2 else dt_out.at[0]
            recv = t_recv.at[kind, x] if kind < 2 else t_recv.at[2, 0]
            return src, dst, t_send.at[kind * 16 + g * 4 + j], recv, dest(kind, g, j), me

        for use in (push, sent):
            for kind, g, j in every:
                if kind == 2:
                    @pl.when(x == 1)
                    def _(g=g, j=j, use=use):
                        use(*spread(2, g, j))
                else:
                    use(*spread(kind, g, j))

        for part in range(2):
            @pl.when(source & (y % 2 == part))
            def _(part=part):
                for k in (1, 2, 3):
                    sent(*ab_args(k, part))

        @pl.when(c_source)
        def _():
            for k in (1, 2, 3):
                sent(*c_args(k))

    for k, pair in enumerate(pairs):
        arrived(ct_out.at[k], ct_send.at[0], ct_recv.at[k], ct_source(*pair), me)

    @pl.when(x > z)
    def _():
        for hop in hops:
            sent(*ct_args(*hop))

    for b in range(4):
        arrived(d_out.at[b], t_send.at[0], t_recv.at[0, b], at(b, y), me)
        arrived(g_out.at[b], t_send.at[0], t_recv.at[1, b], at(b, z), me)
    arrived(dt_out.at[0], t_send.at[0], t_recv.at[2, 0], at(1, z), me)


NAMES = ("stage0", "w_half", "y_half", "h_half", "w_full", "y_full", "h_full", "final")


def vmem_call(kernel, outs, scratch, count, flops, name):
    spec = pl.BlockSpec(memory_space=pltpu.VMEM)
    return pl.pallas_call(
        kernel,
        out_shape=[jax.ShapeDtypeStruct(s, F32) for s in outs],
        in_specs=[spec] * count,
        out_specs=[spec] * len(outs),
        scratch_shapes=scratch,
        compiler_params=pltpu.CompilerParams(has_side_effects=True, vmem_limit_bytes=VMEM_LIMIT, collective_id=NAMES.index(name)),
        cost_estimate=pl.CostEstimate(flops=flops, bytes_accessed=8 << 20, transcendentals=0),
        name=name,
    )


def stage0(l_blk, lt_blk, n):
    big, half, quarter, tile = n // 8, n // 16, n // 32, n // 128
    dma = pltpu.SemaphoreType.DMA
    scratch = [
        pltpu.VMEM((big, half), F32), pltpu.VMEM((half, half), F32), pltpu.VMEM((2, big, half), F32),
        pltpu.VMEM((big, big), F32), pltpu.VMEM((big, big), F32), pltpu.VMEM((big, big), F32),
        pltpu.VMEM((quarter, 2 * big), F32), pltpu.VMEM((quarter, 2 * big), F32), pltpu.VMEM((quarter, 2 * big), F32),
        dma((16,)), dma((6,)), dma((3,)), dma((2,)), dma((3,)), dma((2,)), dma((4,)), dma((4,)), dma((48,)), dma((3, 4)),
    ]
    outs = [(6, tile, half), (4, tile, half), (4, tile, half), (1, tile, half)]
    call = vmem_call(functools.partial(stage0_kernel, n), outs, scratch, 2, 10 ** 10, "stage0")
    return call(l_blk, lt_blk)


def along(axis):
    def to(me, k):
        return dict(me, **{axis: jnp.int32(k)})

    return to, to, lambda me: me[axis]


ALONG = {axis: along(axis) for axis in ("x", "y", "z")}


def mapped(to, source, slot):
    return (lambda me, k: dict(to(me, k), e=me["e"]), lambda me, k: dict(source(me, k), e=me["e"]), slot)


W_TURN = mapped(
    lambda m, k: {"x": jnp.int32(k), "y": m["z"], "z": m["x"]},
    lambda m, k: {"x": m["z"], "y": jnp.int32(k), "z": m["y"]}, lambda m: m["y"])
H_TURN = mapped(
    lambda m, k: {"x": jnp.int32(k), "y": m["x"], "z": m["z"]},
    lambda m, k: {"x": m["y"], "y": jnp.int32(k), "z": m["z"]}, lambda m: m["y"])
Y_TURN = mapped(
    lambda m, k: {"x": jnp.int32(k), "y": m["x"], "z": m["y"]},
    lambda m, k: {"x": m["y"], "y": m["z"], "z": jnp.int32(k)}, lambda m: m["z"])
YT_TURN = mapped(
    lambda m, k: {"x": jnp.int32(k), "y": m["y"], "z": m["x"]},
    lambda m, k: {"x": m["z"], "y": m["y"], "z": jnp.int32(k)}, lambda m: m["z"])


def product_kernel(n, spec, *refs):
    pieces, ops, prods, axis, negate = spec
    tile, half = n // 128, n // 16
    count, made = len(pieces), len(prods)
    ins, outs = refs[:count], refs[count:count + made]
    rest = refs[count + made:]
    bufs, rest = rest[:len(ops)], rest[len(ops):]
    parts, rest = rest[:made], rest[made:]
    sibs, rest = rest[:made], rest[made:]
    adds, rest = rest[:made], rest[made:]
    lands, rest = rest[:made], rest[made:]
    g_send, g_recv, s_send, s_recv, r_send, r_recv = rest
    me = coords()
    e = me["e"]
    sib = dict(me, e=1 - e)

    def piece_args(p, k):
        op, (to, _, slot), down, across, wide = pieces[p]
        at = slot(me)
        dst = bufs[op].at[at, down, :, pl.ds(across * half, wide * half)]
        return ins[p].at[0] if len(ins[p].shape) == 3 else ins[p], dst, g_send.at[p, k], g_recv.at[p, at], to(me, k), me

    maps = {id(p[1]): p[1] for p in pieces}
    maps[id(ALONG[axis])] = ALONG[axis]
    meet([(None, m[1](me, k)) for m in maps.values() for k in range(4)] + [(None, sib)],
         [(None, m[0](me, k)) for m in maps.values() for k in range(4)] + [(None, sib)], me)
    for op, (down, across) in enumerate(ops):
        filled = {(d, a + i) for o, _, d, a, w in pieces if o == op for i in range(w)}
        for d in range(down):
            for a in range(across):
                if (d, a) not in filled:
                    bufs[op][:, d, :, a * half:(a + 1) * half] = jnp.zeros((4, tile, half), F32)
    for p in range(count):
        for k in range(4):
            push(*piece_args(p, k))
    for p in range(count):
        op, (_, source, _), down, across, wide = pieces[p]
        for k in range(4):
            dst = bufs[op].at[k, down, :, pl.ds(across * half, wide * half)]
            arrived(dst, g_send.at[p, 0], g_recv.at[p, k], source(me, k), me)

    def sib_args(q, d, core):
        rows = pl.ds(d * half + core * (half // 2), half // 2)
        return parts[q].at[rows, :], sibs[q].at[d], s_send.at[q, d], s_recv.at[q, d], sib, me

    for q, (lo, ro, down) in enumerate(prods):
        lhs = bufs[lo][...].reshape(-1, bufs[lo].shape[-1])
        rhs = bufs[ro][...].reshape(-1, bufs[ro].shape[-1])
        for d in range(down):
            parts[q][d * half:(d + 1) * half, :] = mm(lhs[:, d * half:(d + 1) * half], rhs, ((0,), (0,)))
            push(parts[q].at[pl.ds((1 - e) * (half // 2) + d * half, half // 2), :], sibs[q].at[d],
                 s_send.at[q, d], s_recv.at[q, d], sib, me)

    def red_args(q, k):
        at = me[axis]
        return adds[q].at[k], lands[q].at[at], r_send.at[q, k], r_recv.at[q, at], dict(me, **{axis: jnp.int32(k)}), me

    for q, (_, _, down) in enumerate(prods):
        for d in range(down):
            arrived(sibs[q].at[d], s_send.at[q, d], s_recv.at[q, d], sib, me)
            first = pl.multiple_of(e * (half // 2) + d * half, 8)
            for k in range(4):
                own = parts[q][pl.ds(first + k * tile, tile), :]
                adds[q][k, d] = own + sibs[q][d, k * tile:(k + 1) * tile, :]
        for k in range(4):
            push(*red_args(q, k))
    for q, (_, _, down) in enumerate(prods):
        for k in range(4):
            arrived(lands[q].at[k], r_send.at[q, k], r_recv.at[q, k], dict(me, **{axis: jnp.int32(k)}), me)
        total = lands[q][0] + lands[q][1] + lands[q][2] + lands[q][3]
        outs[q][...] = -total if negate[q] else total

    for p in range(count):
        for k in range(4):
            sent(*piece_args(p, k))
    for q, (_, _, down) in enumerate(prods):
        for d in range(down):
            push_args = (parts[q].at[pl.ds((1 - e) * (half // 2) + d * half, half // 2), :], sibs[q].at[d],
                         s_send.at[q, d], s_recv.at[q, d], sib, me)
            sent(*push_args)
        for k in range(4):
            sent(*red_args(q, k))


def product(n, pieces, ops, prods, axis, negate, name):
    tile, half = n // 128, n // 16
    dma = pltpu.SemaphoreType.DMA
    arrays = [p[0] for p in pieces]
    table = [(p[1], p[2], p[3], p[4], p[0].shape[-1] // half) for p in pieces]
    widths = [ops[ro][1] * half for _, ro, _ in prods]
    downs = [d for _, _, d in prods]
    scratch = [pltpu.VMEM((4, d, tile, a * half), F32) for d, a in ops]
    scratch += [pltpu.VMEM((d * half, w), F32) for d, w in zip(downs, widths)]
    scratch += [pltpu.VMEM((d, half // 2, w), F32) for d, w in zip(downs, widths)]
    scratch += [pltpu.VMEM((4, d, tile, w), F32) for d, w in zip(downs, widths)] * 2
    top = max(downs)
    scratch += [dma((len(pieces), 4)), dma((len(pieces), 4)), dma((len(prods), top)), dma((len(prods), top)),
                dma((len(prods), 4)), dma((len(prods), 4))]
    outs = [(d, tile, w) for d, w in zip(downs, widths)]
    kernel = functools.partial(product_kernel, n, (table, ops, prods, axis, negate))
    return vmem_call(kernel, outs, scratch, len(arrays), 3 * 10 ** 9, name)(*arrays)


def final_kernel(n, plan, *refs):
    tile, half, big = n // 128, n // 16, n // 8
    count = len(plan)
    ins, out = refs[:count], refs[count]
    flat, extra, turned, f_send, f_recv, a_recv, u_recv = refs[count + 1:]
    me = coords()
    x, y, z, e = me["x"], me["y"], me["z"], me["e"]

    def args(p):
        b_row, b_col, kind, rax, cax, gax = plan[p]
        a_r, a_c, g = me[rax], me[cax], me[gax]
        if kind == "turn":
            dst = turned.at[pl.ds(pl.multiple_of(e * (half // 2) + g * tile, 8), tile), pl.ds(pl.multiple_of((a_c % 2) * half, half), half)]
            to = {"x": jnp.int32(b_col), "y": a_r, "z": jnp.int32(b_row), "e": a_c // 2}
            return ins[p], dst, f_send.at[p], u_recv.at[a_c % 2, g, e], to, me
        rows = pl.ds(pl.multiple_of((a_r % 2) * half + e * (half // 2) + g * tile, 8), tile)
        to = {"x": jnp.int32(b_row), "y": a_c, "z": jnp.int32(b_col), "e": a_r // 2}
        if kind == "add":
            return ins[p], extra.at[rows, :], f_send.at[p], a_recv.at[a_r % 2, g, e], to, me
        return ins[p], flat.at[rows, :], f_send.at[p], f_recv.at[a_r % 2, g, e], to, me

    def incoming(p):
        b_row, b_col, kind, rax, cax, gax = plan[p]
        to_x, to_z = (b_col, b_row) if kind == "turn" else (b_row, b_col)
        found = []
        for h in range(2):
            a_r, a_c = (y, 2 * e + h) if kind == "turn" else (2 * e + h, y)
            found += [{rax: a_r, cax: a_c, gax: jnp.int32(g), "e": jnp.int32(ee)} for g in range(4) for ee in range(2)]
        return (x == to_x) & (z == to_z), found

    sources = []
    for p in range(count):
        cond, found = incoming(p)
        sources += [(cond, at) for at in found]
    meet(sources, [(None, args(p)[4]) for p in range(count)], me)
    for p in range(count):
        push(*args(p))
    for p in range(count):
        kind = plan[p][2]
        cond, found = incoming(p)

        @pl.when(cond)
        def _(kind=kind, found=found):
            for h in range(2):
                for g in range(4):
                    for ee in range(2):
                        first = ee * (half // 2) + g * tile
                        if kind == "turn":
                            dst, sem = turned.at[pl.ds(first, tile), pl.ds(h * half, half)], u_recv.at[h, g, ee]
                        else:
                            dst = (extra if kind == "add" else flat).at[pl.ds(h * half + first, tile), :]
                            sem = (a_recv if kind == "add" else f_recv).at[h, g, ee]
                        arrived(dst, f_send.at[0], sem, found[h * 8 + g * 2 + ee], me)

    adds = {(p[0], p[1]) for p in plan if p[2] == "add"}
    turns = {(p[1], p[0]) for p in plan if p[2] == "turn"}
    keeps = {(p[0], p[1]) for p in plan if p[2] == "keep"}
    for b_row in range(4):
        for b_col in range(4):
            @pl.when((x == b_row) & (z == b_col))
            def _(at=(b_row, b_col)):
                total = None
                if at in keeps:
                    total = flat[...]
                if at in adds:
                    total = extra[...] if total is None else total + extra[...]
                if at in turns:
                    moved = turned[...].T
                    total = moved if total is None else total + moved
                out[...] = total
    for p in range(count):
        sent(*args(p))


def final(n, items):
    tile, half, big = n // 128, n // 16, n // 8
    dma = pltpu.SemaphoreType.DMA
    arrays = [i[0] for i in items]
    plan = [i[1:] for i in items]
    scratch = [pltpu.VMEM((big, half), F32), pltpu.VMEM((big, half), F32), pltpu.VMEM((half, big), F32),
               dma((len(items),)), dma((2, 4, 2)), dma((2, 4, 2)), dma((2, 4, 2))]
    call = vmem_call(functools.partial(final_kernel, n, plan), [(big, half)], scratch, len(arrays), 10 ** 7, "final")
    return call(*arrays)[0]


def solution(mesh):
    def local_fn(l_blk):
        n = l_blk.shape[0] * 8
        half = n // 16
        ct, d, g, dt = stage0(l_blk, l_blk.T, n)
        dt = dt[0]
        ct = {(r, c): ct[(r * (r - 1)) // 2 + c] for r in range(4) for c in range(r)}
        ax, ay, az = ALONG["x"], ALONG["y"], ALONG["z"]

        def piece(array, op, how, down=0, across=0):
            return array, op, how, down, across

        def part(array, r, c):
            return array[r][:, c * half:(c + 1) * half]

        one, two, minus = (1, 1), (2, 2), (True,) * 3
        (w0,), (w1,) = product(
            n, [piece(ct[1, 0], 0, ax), piece(d[0], 1, az), piece(ct[3, 2], 2, ax), piece(d[2], 3, az)],
            [one] * 4, [(0, 1, 1), (2, 3, 1)], "y", (False,) * 2, "w_half")
        (y0, x21), (y1,), (yt1,) = product(
            n, [piece(g[1], 0, ax), piece(dt, 0, ax, 0, 1), piece(w0, 1, ay), piece(g[3], 2, ax), piece(w1, 3, ay)],
            [(1, 2), one, one, one], [(0, 1, 2), (2, 3, 1), (3, 2, 1)], "z", minus, "y_half")
        (h0,), (h1,) = product(
            n, [piece(w0, 0, W_TURN), piece(y0, 1, az), piece(w1, 2, W_TURN), piece(y1, 3, az)],
            [one] * 4, [(0, 1, 1), (2, 3, 1)], "y", minus, "h_half")
        g0, g2 = g[0] + h0, g[2] + h1
        whole = [(0, 1, 2)]
        (w,) = product(
            n, [piece(ct[2 + r, c], 0, ax, c, r) for r in range(2) for c in range(2)]
            + [piece(d[0], 1, az), piece(jnp.concatenate([x21, d[1]], axis=1), 1, az, 1)],
            [two] * 2, whole, "y", (False,), "w_full")
        (yy,) = product(
            n, [piece(g2, 0, H_TURN), piece(yt1, 0, YT_TURN, 0, 1), piece(y1, 0, Y_TURN, 1), piece(g[3], 0, ax, 1, 1)]
            + [piece(w[r], 1, ay, r) for r in range(2)],
            [two] * 2, whole, "z", minus, "y_full")
        (h,) = product(
            n, [piece(w[r], 0, W_TURN, r) for r in range(2)] + [piece(yy[r], 1, az, r) for r in range(2)],
            [two] * 2, whole, "y", minus, "h_full")
        items = []
        for r in range(2):
            for c in range(2):
                items.append((part(h, r, c), r, c, "keep", *"zxy"))
                items += [(part(yy, r, c), 2 + r, c, kind, *"yxz") for kind in ("keep", "turn")]
        items += [(g0, 0, 0, "add", *"zxy"), (g[1], 1, 1, "add", *"zyx"), (g2, 2, 2, "keep", *"zxy"),
                  (g[3], 3, 3, "keep", *"zyx")]
        for array, r, keep in ((y0, 1, "add"), (y1, 3, "keep")):
            items += [(array, r, r - 1, kind, *"yxz") for kind in (keep, "turn")]
        return final(n, items)

    spec = P(("batch", "row"), "col")
    return jax.shard_map(local_fn, mesh=mesh, in_specs=(spec,), out_specs=spec, check_vma=False)
```

time: 1500 us -> 488 us (0.33)
  the two profiles are of different devices: /device:TPU:1 before, /device:TPU:33 now
where the time goes in v1:
time: 488 us; the launch traced here: 480 us
  Pallas kernels  460 us (94%)
  local copies, waits for them, and re-layouts  17.2 us (4%)
    pallas_call x6, Pallas kernels, product(): vmem_call(kernel, outs, scratch, len(arrays), 3 * 10 ** 9, name)(*arrays)  307 us
    pallas_call x1, Pallas kernels, stage0(): return call(l_blk, lt_blk)  90.4 us
    pallas_call x1, Pallas kernels, final(): return call(*arrays)[0]  62.5 us

profile of v1, /device:TPU:33, one launch (start us, length us, event | category | flops | bytes accessed | tf_op | source)
XLA Modules:
  0.0 479.7 jit_solution(11907677896701846845)
XLA Ops:
  0.0 2.7 copy.2
  2.7 90.4 %stage0.1 = (f32[6,48,384]{2,1,0:T(8,128)}, f32[4,48,384]{2,1,0:T(8,128)}, f32[4,48,384]{2,1,0:T(8,128)}, f32[1,48,384]{2,1,0:T(8,128)}) custom-call(f32[768,384]{1,0:T(8,128)} %l_ref.1, f32[384,768]{1,0:T(8,128)} %bitcast.48), custom_call_target="tpu_custom_call" | custom-call | flops 10000000000 | bytes 8388608 | tf_op jit(solution)/shard_map/stage0/pallas_call | solution.py:335
  93.1 1.8 slice_bitcast_fusion.11
  94.9 1.8 slice_bitcast_fusion.9
  96.6 62.2 %w_half.1 = (f32[1,48,384]{2,1,0:T(8,128)}, f32[1,48,384]{2,1,0:T(8,128)}) custom-call(f32[48,384]{1,0:T(8,128)} %get-tuple-element.28.refs_0_, f32[48,384]{1,0:T(8,128)} %get-tuple-element.56.refs_1_.refs_4_, f32[48,384]{1,0:T(8,128)} %get-tuple-element.27.refs_2_, f32[48,384]{1,0:T(8,128)} %get-tuple-element.58.refs_3_), custom_call_target="tpu_custom_call" | custom-call | flops 3000000000 | bytes 8388608 | tf_op jit(solution)/shard_map/w_half/pallas_call | solution.py:466
  158.9 36.2 %y_half.1 = (f32[2,48,384]{2,1,0:T(8,128)}, f32[1,48,384]{2,1,0:T(8,128)}, f32[1,48,384]{2,1,0:T(8,128)}) custom-call(f32[48,384]{1,0:T(8,128)} %get-tuple-element.42.refs_0_.refs_13_, f32[48,384]{1,0:T(8,128)} %bitcast.58, f32[48,384]{1,0:T(8,128)} %bitcast.54, f32[48,384]{1,0:T(8,128)} %get-tuple-element.41.refs_3_.refs_15_, f32[48,384]{1,0:T(8,128)} %bitcast.56), custom_call_target="tpu_custom_call" | custom-call | flops 3000000000 | bytes 8388608 | tf_op jit(solution)/shard_map/y_half/pallas_call | solution.py:466
  195.1 1.6 slice_bitcast_fusion.6
  196.6 0.7 pad_maximum_fusion.refs_5_
  197.3 39.9 %w_full.1 = f32[2,48,768]{2,1,0:T(8,128)} custom-call(f32[48,384]{1,0:T(8,128)} %get-tuple-element.32.refs_0_, f32[48,384]{1,0:T(8,128)} %get-tuple-element.31.refs_1_, f32[48,384]{1,0:T(8,128)} %get-tuple-element.30.refs_2_, f32[48,384]{1,0:T(8,128)} %get-tuple-element.29.refs_3_, f32[48,384]{1,0:T(8,128)} %get-tuple-element.56.refs_1_.refs_4_, ...), custom_call_target="tpu_custom_call" | custom-call | flops 3000000000 | bytes 8388608 | tf_op jit(solution)/shard_map/w_full/pallas_call | solution.py:466
  237.2 1.7 slice_bitcast_fusion.4
  238.9 38.5 %h_half.1 = (f32[1,48,384]{2,1,0:T(8,128)}, f32[1,48,384]{2,1,0:T(8,128)}) custom-call(f32[48,384]{1,0:T(8,128)} %bitcast.55, f32[48,384]{1,0:T(8,128)} %get-tuple-element.54.refs_1_.refs_16_.refs_17_, f32[48,384]{1,0:T(8,128)} %bitcast.57, f32[48,384]{1,0:T(8,128)} %bitcast.49), custom_call_target="tpu_custom_call" | custom-call | flops 3000000000 | bytes 8388608 | tf_op jit(solution)/shard_map/h_half/pallas_call | solution.py:466
  277.4 0.0 copy-done.2
  277.4 1.6 add_bitcast_fusion
  279.0 58.7 %y_full.1 = f32[2,48,768]{2,1,0:T(8,128)} custom-call(f32[48,384]{1,0:T(8,128)} %get-tuple-element.34.refs_0_.refs_14_, f32[48,384]{1,0:T(8,128)} %bitcast.53, f32[48,384]{1,0:T(8,128)} %bitcast.50, f32[48,384]{1,0:T(8,128)} %get-tuple-element.41.refs_3_.refs_15_, f32[48,768]{1,0:T(8,128)} %get-tuple-element.40.refs_4_.refs_0_, ...), custom_call_target="tpu_custom_call" | custom-call | flops 3000000000 | bytes 8388608 | tf_op jit(solution)/shard_map/y_full/pallas_call | solution.py:466
  337.7 1.7 slice_bitcast_fusion.2
  339.4 71.2 %h_full.1 = f32[2,48,768]{2,1,0:T(8,128)} custom-call(f32[48,768]{1,0:T(8,128)} %get-tuple-element.40.refs_4_.refs_0_, f32[48,768]{1,0:T(8,128)} %get-tuple-element.39.refs_5_.refs_1_, f32[48,768]{1,0:T(8,128)} %get-tuple-element.38.refs_2_, f32[48,768]{1,0:T(8,128)} %get-tuple-element.37.refs_3_), custom_call_target="tpu_custom_call" | custom-call | flops 3000000000 | bytes 8388608 | tf_op jit(solution)/shard_map/h_full/pallas_call | solution.py:466
  410.7 0.0 copy-done.1
  410.7 0.7 fusion
  411.3 0.7 fusion.2
  412.0 1.0 slice_bitcast_fusion
  413.0 0.7 fusion.1
  413.7 0.7 fusion.3
  414.3 62.5 %final.1 = f32[768,384]{1,0:T(8,128)} custom-call(f32[48,384]{1,0:T(8,128)} %get-tuple-element.53.refs_0_, f32[48,384]{1,0:T(8,128)} %get-tuple-element.51.refs_1_.refs_2_, f32[48,384]{1,0:T(8,128)} %get-tuple-element.51.refs_1_.refs_2_, f32[48,384]{1,0:T(8,128)} %get-tuple-element.52.refs_3_, f32[48,384]{1,0:T(8,128)} %get-tuple-element.50.refs_4_.refs_5_, ...), custom_call_target="tpu_custom_call" | custom-call | flops 10000000 | bytes 8388608 | tf_op jit(solution)/shard_map/final/pallas_call | solution.py:551
  476.9 2.4 copy.4
  (4 shorter events, 0.0 us)
Async XLA Ops:
  238.9 38.5 %copy-start.2 = (f32[4,48,384]{2,1,0:T(8,128)S(1)}, f32[4,48,384]{2,1,0:T(8,128)}, u32[]{:S(2)}) copy-start(f32[4,48,384]{2,1,0:T(8,128)} %get-tuple-element.18) | copy-start | bytes 884740
  339.4 71.2 %copy-start.1 = (f32[48,768]{1,0:T(8,128)S(1)}, f32[48,768]{1,0:T(8,128)}, u32[]{:S(2)}) copy-start(f32[48,768]{1,0:T(8,128)} %get-tuple-element.37.refs_3_) | copy-start | bytes 442372
  339.4 71.9 %copy-start = (f32[48,768]{1,0:T(8,128)S(1)}, f32[48,768]{1,0:T(8,128)}, u32[]{:S(2)}) copy-start(f32[48,768]{1,0:T(8,128)} %get-tuple-element.38.refs_2_) | copy-start | bytes 442372
